TPU v7x, 32 devices: a whole 2x2x4 slice. The times are simulated.
32 devices in a mesh: vocab: 16 (over z, x, core), seq: 2 (over y).
Axes of the slice: x: 2, y: 2, z: 4, core: 2. Of those that a mesh axis runs over, the one named last changes fastest.
Arguments:
- hidden_states: bfloat16 [512, 3584], P('seq', 'vocab'), may hold values from -6 to 6
- norm_gain: float32 [3584], replicated, may hold values from 0.5 to 1.5
- embedding: bfloat16 [256000, 3584], P(('vocab', 'seq')), may hold values from -0.29882812 to 0.29882812
- targets: int32 [512], replicated, may hold values from 0 to 255999
Outputs:
- token_loss: float32 [512], P('seq')
- mean_loss: float32 [], replicated
All inputs are finite; a program needn't handle non-finite values.
Results may differ from a plain program's by a relative error of at most 0.0005.
Values may be sent and summed in bfloat16 or wider, within the bound.
A program may use at most 128 MiB of HBM per device.

v0:
```python
import jax
import jax.numpy as jnp
from jax import lax
from jax.sharding import PartitionSpec as P


def normalize(rows, norm_gain):
    values = rows.astype(jnp.float32)
    meansq = jnp.mean(values * values, axis=-1, keepdims=True)
    return (values * lax.rsqrt(meansq + 1e-06) * norm_gain).astype(jnp.bfloat16)


def vocab_terms_of(embedding, targets, normed_rows):
    local_rows = embedding.shape[0]
    base = (lax.axis_index("vocab") * lax.axis_size("seq") + lax.axis_index("seq")) * local_rows
    scores = jnp.einsum("vd,td->vt", embedding, normed_rows, preferred_element_type=jnp.float32)
    capped = 30.0 * jnp.tanh(scores / 30.0)
    total = jnp.sum(jnp.exp(capped), axis=0)
    ids = base + jnp.arange(local_rows, dtype=jnp.int32)
    hit = ids[:, None] == targets[None, :]
    picked = jnp.sum(jnp.where(hit, capped, 0.0), axis=0)
    return (total, picked)


def local(hidden_states, norm_gain, embedding, targets):
    own_count = hidden_states.shape[0]
    all_count = targets.shape[0]
    gathered_rows = lax.all_gather(hidden_states, "seq", axis=0, tiled=True)
    whole = lax.all_gather(gathered_rows, "vocab", axis=1, tiled=True)
    normed = normalize(whole, norm_gain)
    total, picked = vocab_terms_of(embedding, targets, normed)
    total, picked = lax.psum((total, picked), ("vocab", "seq"))
    every_loss = jnp.log(total) - picked
    mean_loss = jnp.sum(every_loss) / all_count
    token_loss = lax.dynamic_slice_in_dim(every_loss, lax.axis_index("seq") * own_count, own_count)
    return (token_loss, mean_loss)


def solution(mesh):
    placed = (P("seq", "vocab"), P(), P(("vocab", "seq"), None), P())
    return jax.shard_map(
        local, mesh=mesh, in_specs=placed, out_specs=(P("seq"), P()), check_vma=False
    )
```

profile of v0, /device:TPU:0, one launch (start us, length us, event | category | flops | bytes accessed | tf_op | source)
XLA Modules:
  0.0 157.3 jit_solution(12015956932428505481)
XLA Ops:
  7.2 0.0 all-gather.2.cloned.1.call-start
  7.2 8.7 %all_gather.6 = bf16[512,224]{0,1:T(8,128)(2,1)} all-gather(bf16[256,224]{0,1:T(8,128)(2,1)} %param.4), channel_id=1, replica_groups=mesh['vocab'=16,'seq'=2] {'seq'}, dimensions={0}, use_global_device_ids=true | all-gather | bytes 344064 | tf_op jit(solution)/shard_map/all_gather | solution.py:28
  15.9 0.0 all-gather.2.cloned.1.call-update
  15.9 48.1 %all-gather.2.cloned.1.call-done = bf16[512,3584]{0,1:T(8,128)(2,1)} async-done(((bf16[512,224]{0,1:T(8,128)(2,1)}), bf16[512,3584]{0,1:T(8,128)(2,1)}) %all-gather.2.cloned.1.call-update) | async-done | bytes 3670032 | tf_op jit(solution)/shard_map/all_gather | solution.py:29
  64.0 2.9 %fusion.2 = f32[512]{0:T(512)S(1)} fusion(bf16[512,3584]{0,1:T(8,128)(2,1)} %all-gather.2.cloned.1.call-done), kind=kLoop, calls=%fused_computation.7 | loop fusion | flops 5504512 | bytes 3672064 | tf_op jit(solution)/shard_map/reduce_sum | solution.py:9
  66.9 41.1 %fusion = (f32[512]{0:T(512)S(1)}, f32[512]{0:T(512)S(1)}) fusion(s32[512]{0:T(512)} %param.7, s32[8000]{0:T(1024)S(1)} %iota_add_fusion, bf16[8000,3584]{1,0:T(8,128)(2,1)} %param.6, bf16[512,3584]{0,1:T(8,128)(2,1)} %all-gather.2.cloned.1.call-done, f32[3584]{0:T(1024)} %param.5, f32[512]{0:T(512)S(1)} %add_rsqrt_fusion), kind=kOutput, calls=%fused_computation.2 | convolution fusion | flops 29392044032 | bytes 61068544 | tf_op jit(solution)/shard_map/vd,td->vt/dot_general | solution.py:16
  108.0 39.4 %all-reduce = (f32[512]{0:T(512)S(1)}, f32[512]{0:T(512)S(1)}) all-reduce(f32[512]{0:T(512)S(1)} %get-tuple-element.3, f32[512]{0:T(512)S(1)} %get-tuple-element.2), channel_id=1, replica_groups=mesh['vocab'=16,'seq'=2] {'vocab','seq'}, use_global_device_ids=true, to_apply=%region_4.5 | all-reduce | flops 1024 | bytes 8192 | tf_op jit(solution)/shard_map/psum | solution.py:32
  147.4 0.6 fusion.8
  148.7 0.6 dynamic_slice.3
  (2 shorter events, 0.0 us)
Async XLA Ops:
  7.2 56.8 %all-gather.2.cloned.1.call-start = ((), (), s32[]{:S(2)}) async-start(), calls=%async_computation | async-start | bytes 3899392 | tf_op jit(solution)/shard_map/all_gather | solution.py:29
Sparse Core Ops, SparseCore 0:
  16.0 47.9 all-gather.1
where the time goes:
time: 158 us; the launch traced here: 157 us
  blocking collectives  48.1 us (30%)
  waiting for transfers between devices  48.1 us (30%)
  matrix products  41.1 us (26%)
  between operations  15.8 us (10%)
  other arithmetic  3.5 us (2%)
    all_gather x1, waiting for transfers between devices, local(): whole = lax.all_gather(gathered_rows, 'vocab', axis=1, tiled=True)  48.1 us
    dot_general x1, matrix products, vocab_terms_of(): jnp.einsum('vd,td->vt', embedding, normed_rows, preferred_element_type=jn...  41.1 us
    psum x1, blocking collectives, local(): total, picked = lax.psum((total, picked), ('vocab', 'seq'))  39.4 us
    all_gather x1, blocking collectives, local(): gathered_rows = lax.all_gather(hidden_states, 'seq', axis=0, tiled=True)  8.67 us
  transfers between devices with their start and end apart: 1, of which 1 were waited for; matrix products, arithmetic and copies ran while one was open for 0% of the time, Pallas kernels for 0%

commit v1 on v0

--- a/solution.py
+++ b/solution.py
@@ -2,6 +2,11 @@
 import jax.numpy as jnp
 from jax import lax
 from jax.sharding import PartitionSpec as P
+
+
+def drive_shelves(m):
+    front = lax.psum(m, "seq")
+    return lax.psum(front, "vocab")
 
 
 def normalize(rows, norm_gain):
@@ -29,7 +34,7 @@
     whole = lax.all_gather(gathered_rows, "vocab", axis=1, tiled=True)
     normed = normalize(whole, norm_gain)
     total, picked = vocab_terms_of(embedding, targets, normed)
-    total, picked = lax.psum((total, picked), ("vocab", "seq"))
+    total, picked = drive_shelves((total, picked))
     every_loss = jnp.log(total) - picked
     mean_loss = jnp.sum(every_loss) / all_count
     token_loss = lax.dynamic_slice_in_dim(every_loss, lax.axis_index("seq") * own_count, own_count)

time: 158 us -> 153 us (0.968)
  blocking collectives: 48.1 us -> 43.8 us
    psum x1 -> x2, blocking collectives: 39.4 us -> 35.1 us  [the longest x1 30.2 us: drive_shelves(): return lax.psum(front, 'vocab')]
where the time goes in v1:
time: 153 us
  waiting for transfers between devices  48.1 us (31%)
  blocking collectives  43.8 us (29%)
  matrix products  41.1 us (27%)
  between operations  15.8 us (10%)
  other arithmetic  3.5 us (2%)
    all_gather x1, waiting for transfers between devices, local(): whole = lax.all_gather(gathered_rows, 'vocab', axis=1, tiled=True)  48.1 us
    dot_general x1, matrix products, vocab_terms_of(): jnp.einsum('vd,td->vt', embedding, normed_rows, preferred_element_type=jn...  41.1 us
    psum x1, blocking collectives, drive_shelves(): return lax.psum(front, 'vocab')  30.2 us
    all_gather x1, blocking collectives, local(): gathered_rows = lax.all_gather(hidden_states, 'seq', axis=0, tiled=True)  8.67 us
    psum x1, blocking collectives, drive_shelves(): front = lax.psum(m, 'seq')  4.93 us
  transfers between devices with their start and end apart: 1, of which 1 were waited for; matrix products, arithmetic and copies ran while one was open for 0% of the time, Pallas kernels for 0%

profile of v1, /device:TPU:0, one launch (start us, length us, event | category | flops | bytes accessed | tf_op | source)
XLA Modules:
  0.0 153.0 jit_solution(10168680514422203857)
XLA Ops:
  7.2 0.0 all-gather.2.cloned.1.call-start
  7.2 8.7 %all_gather.6 = bf16[512,224]{0,1:T(8,128)(2,1)} all-gather(bf16[256,224]{0,1:T(8,128)(2,1)} %param.4), channel_id=1, replica_groups=mesh['vocab'=16,'seq'=2] {'seq'}, dimensions={0}, use_global_device_ids=true | all-gather | bytes 344064 | tf_op jit(solution)/shard_map/all_gather | solution.py:33
  15.9 0.0 all-gather.2.cloned.1.call-update
  15.9 48.1 %all-gather.2.cloned.1.call-done = bf16[512,3584]{0,1:T(8,128)(2,1)} async-done(((bf16[512,224]{0,1:T(8,128)(2,1)}), bf16[512,3584]{0,1:T(8,128)(2,1)}) %all-gather.2.cloned.1.call-update) | async-done | bytes 3670032 | tf_op jit(solution)/shard_map/all_gather | solution.py:34
  64.0 2.9 %fusion.2 = f32[512]{0:T(512)S(1)} fusion(bf16[512,3584]{0,1:T(8,128)(2,1)} %all-gather.2.cloned.1.call-done), kind=kLoop, calls=%fused_computation.7 | loop fusion | flops 5504512 | bytes 3672064 | tf_op jit(solution)/shard_map/reduce_sum | solution.py:14
  66.9 41.1 %fusion = (f32[512]{0:T(512)S(1)}, f32[512]{0:T(512)S(1)}) fusion(s32[512]{0:T(512)} %param.7, s32[8000]{0:T(1024)S(1)} %iota_add_fusion, bf16[8000,3584]{1,0:T(8,128)(2,1)} %param.6, bf16[512,3584]{0,1:T(8,128)(2,1)} %all-gather.2.cloned.1.call-done, f32[3584]{0:T(1024)} %param.5, f32[512]{0:T(512)S(1)} %add_rsqrt_fusion), kind=kOutput, calls=%fused_computation.2 | convolution fusion | flops 29392044032 | bytes 61068544 | tf_op jit(solution)/shard_map/vd,td->vt/dot_general | solution.py:21
  108.0 4.9 %all-reduce.1 = (f32[512]{0:T(512)S(1)}, f32[512]{0:T(512)S(1)}) all-reduce(f32[512]{0:T(512)S(1)} %get-tuple-element.3, f32[512]{0:T(512)S(1)} %get-tuple-element.2), channel_id=1, replica_groups=mesh['vocab'=16,'seq'=2] {'seq'}, use_global_device_ids=true, to_apply=%region_5.6 | all-reduce | flops 1024 | bytes 8192 | tf_op jit(solution)/shard_map/psum | solution.py:8
  113.0 30.2 %all-reduce = (f32[512]{0:T(512)S(1)}, f32[512]{0:T(512)S(1)}) all-reduce(f32[512]{0:T(512)S(1)} %get-tuple-element.6, f32[512]{0:T(512)S(1)} %get-tuple-element.7), channel_id=1, replica_groups=mesh['vocab'=16,'seq'=2] {'vocab'}, use_global_device_ids=true, to_apply=%region_6.7 | all-reduce | flops 1024 | bytes 8192 | tf_op jit(solution)/shard_map/psum | solution.py:9
  143.1 0.6 fusion.8
  144.4 0.6 dynamic_slice.3
  (2 shorter events, 0.0 us)
Async XLA Ops:
  7.2 56.8 %all-gather.2.cloned.1.call-start = ((), (), s32[]{:S(2)}) async-start(), calls=%async_computation | async-start | bytes 3899392 | tf_op jit(solution)/shard_map/all_gather | solution.py:34
Sparse Core Ops, SparseCore 0:
  16.0 47.9 all-gather.1
